TPU v7x, 32 devices: a whole 2x2x4 slice. The times are simulated.
32 devices in a mesh: gx: 2 (over y), gy: 4 (over z), gz: 4 (over x, core).
Axes of the slice: x: 2, y: 2, z: 4, core: 2. Of those that a mesh axis runs over, the one named last changes fastest.
Arguments:
- tokens: bfloat16 [512, 6144], P(('gx', 'gy'), 'gz'), may hold values from -6 to 6
- grad_out: bfloat16 [512, 6144], P(('gx', 'gy'), 'gz'), may hold values from -1.5 to 1.5
- w_in: bfloat16 [6144, 12288], P('gz', ('gy', 'gx')), may hold values from -0.078125 to 0.078125
- w_out: bfloat16 [12288, 6144], P(('gy', 'gx'), 'gz'), may hold values from -0.0546875 to 0.0546875
Outputs:
- mlp_out: bfloat16 [512, 6144], P(('gx', 'gy'), 'gz')
- tok_grad: bfloat16 [512, 6144], P(('gx', 'gy'), 'gz')
- win_grad: float32 [6144, 12288], P('gz', ('gy', 'gx'))
- wout_grad: float32 [12288, 6144], P(('gy', 'gx'), 'gz')
All inputs are finite; a program needn't handle non-finite values.
Results may differ from a plain program's by a relative error of at most 0.01.
Values may be sent and summed in bfloat16 or wider, within the bound.
A program may use at most 128 MiB of HBM per device.

v0:
```python
import math

import jax
import jax.numpy as jnp
from jax import lax
from jax.sharding import PartitionSpec as P


def gelu_slope(values):
    cdf = 0.5 * (1.0 + jax.scipy.special.erf(values * 0.7071067811865476))
    density = jnp.exp(-0.5 * values * values) * 0.3989422804014327
    return cdf + values * density


def contract_last(left, right):
    return lax.dot_general(
        left, right, (((1,), (1,)), ((), ())), preferred_element_type=jnp.float32
    )


def contract_first(left, right):
    return lax.dot_general(
        left, right, (((0,), (0,)), ((), ())), preferred_element_type=jnp.float32
    )


def per_device(tokens, grad_out, w_in, w_out):
    tok_rows, grad_rows = (
        lax.all_gather(tokens, "gy", axis=0, tiled=True),
        lax.all_gather(grad_out, "gy", axis=0, tiled=True),
    )
    win_tile, wout_tile = (
        lax.all_gather(w_in, "gx", axis=1, tiled=True),
        lax.all_gather(w_out, "gx", axis=0, tiled=True),
    )
    row_total = tok_rows.shape[0]
    block_scale = 1.0 / math.sqrt(row_total)
    pre_part = lax.psum_scatter(
        jnp.dot(tok_rows, win_tile, preferred_element_type=jnp.float32),
        "gz",
        scatter_dimension=0,
        tiled=True,
    )
    act_part = jax.nn.gelu(pre_part, approximate=False).astype(jnp.bfloat16)
    act_all = lax.all_gather(act_part, "gz", axis=0, tiled=True)
    mlp_out = lax.psum_scatter(
        jnp.dot(act_all, wout_tile, preferred_element_type=jnp.float32),
        "gy",
        scatter_dimension=0,
        tiled=True,
    ).astype(jnp.bfloat16)
    wout_grad = lax.psum_scatter(
        (contract_first(act_all, grad_rows) * block_scale).astype(jnp.bfloat16),
        "gx",
        scatter_dimension=0,
        tiled=True,
    ).astype(jnp.float32)
    dact_part = lax.psum_scatter(
        contract_last(grad_rows, wout_tile), "gz", scatter_dimension=0, tiled=True
    )
    dpre_part = (dact_part * gelu_slope(pre_part)).astype(jnp.bfloat16)
    dpre_all = lax.all_gather(dpre_part, "gz", axis=0, tiled=True)
    tok_grad = lax.psum_scatter(
        contract_last(dpre_all, win_tile), "gy", scatter_dimension=0, tiled=True
    ).astype(jnp.bfloat16)
    win_term = contract_first(tok_rows, dpre_all) * block_scale
    win_grad = lax.psum_scatter(
        win_term.astype(jnp.bfloat16), "gx", scatter_dimension=1, tiled=True
    ).astype(jnp.float32)
    return (mlp_out, tok_grad, win_grad, wout_grad)


def solution(mesh):
    in_specs = (
        P(("gx", "gy"), "gz"),
        P(("gx", "gy"), "gz"),
        P("gz", ("gy", "gx")),
        P(("gy", "gx"), "gz"),
    )
    out_specs = (
        P(("gx", "gy"), "gz"),
        P(("gx", "gy"), "gz"),
        P("gz", ("gy", "gx")),
        P(("gy", "gx"), "gz"),
    )
    return jax.shard_map(
        per_device, mesh=mesh, in_specs=in_specs, out_specs=out_specs, check_vma=False
    )
```

profile of v0, /device:TPU:0, one launch (start us, length us, event | category | flops | bytes accessed | tf_op | source)
XLA Modules:
  0.0 691.5 jit_solution(6097030964073734867)
XLA Ops:
  7.2 0.0 copy-start
  7.2 0.0 all-gather.9.cloned.1.call-start
  7.2 0.7 all-gather.9.cloned.1.call-update
  7.9 0.0 all-gather.5.cloned.1.call-start
  8.0 0.7 all-gather.5.cloned.1.call-update
  8.7 0.0 reduce-scatter.11.cloned.1.call-start
  8.7 0.0 copy-done
  8.7 21.3 %all_gather.22 = bf16[256,1536]{1,0:T(8,128)(2,1)S(1)} all-gather(bf16[64,1536]{1,0:T(8,128)(2,1)S(1)} %copy-done), channel_id=1, replica_groups=mesh['gx'=2,'gy'=4,'gz'=4] {'gy'}, dimensions={0}, use_global_device_ids=true | all-gather | bytes 983040 | tf_op jit(solution)/shard_map/all_gather | solution.py:30
  30.0 0.0 copy-start.1
  30.0 100.3 %all-gather.9.cloned.1.call-done = bf16[3072,1536]{1,0:T(8,128)(2,1)} async-done(((bf16[1536,1536]{1,0:T(8,128)(2,1)}), bf16[3072,1536]{1,0:T(8,128)(2,1)}) %all-gather.9.cloned.1.call-update) | async-done | bytes 9437200 | tf_op jit(solution)/shard_map/all_gather | solution.py:34
  130.3 8.0 %fusion.19 = f32[256,3072]{1,0:T(8,128)} fusion(bf16[256,1536]{1,0:T(8,128)(2,1)S(1)} %all_gather.22, bf16[3072,1536]{1,0:T(8,128)(2,1)} %all-gather.9.cloned.1.call-done), kind=kOutput, calls=%fused_computation.31 | convolution fusion | flops 2415919104 | bytes 13369344 | tf_op jit(solution)/shard_map/dot_general | solution.py:16
  138.3 0.0 reduce-scatter.11.cloned.1.call-update
  138.3 0.0 reduce-scatter.7.cloned.1.call-start
  138.3 0.0 copy-done.1
  138.3 19.6 %all_gather.18 = bf16[256,1536]{1,0:T(8,128)(2,1)S(1)} all-gather(bf16[64,1536]{1,0:T(8,128)(2,1)S(1)} %copy-done.1), channel_id=1, replica_groups=mesh['gx'=2,'gy'=4,'gz'=4] {'gy'}, dimensions={0}, use_global_device_ids=true | all-gather | bytes 983040 | tf_op jit(solution)/shard_map/all_gather | solution.py:29
  157.9 91.9 %all-gather.5.cloned.1.call-done = bf16[1536,3072]{1,0:T(8,128)(2,1)} async-done(((bf16[1536,1536]{1,0:T(8,128)(2,1)}), bf16[1536,3072]{1,0:T(8,128)(2,1)}) %all-gather.5.cloned.1.call-update) | async-done | bytes 9437200 | tf_op jit(solution)/shard_map/all_gather | solution.py:33
  249.8 7.9 %fusion.17 = f32[256,3072]{1,0:T(8,128)} fusion(bf16[256,1536]{1,0:T(8,128)(2,1)S(1)} %all_gather.18, bf16[1536,3072]{1,0:T(8,128)(2,1)} %all-gather.5.cloned.1.call-done), kind=kOutput, calls=%fused_computation.29 | convolution fusion | flops 2415919104 | bytes 13369344 | tf_op jit(solution)/shard_map/dot_general | solution.py:39
  257.8 0.0 reduce-scatter.7.cloned.1.call-update
  257.8 0.0 all-gather.11.cloned.1.call-start
  257.9 33.0 %reduce-scatter.11.cloned.1.call-done = f32[64,3072]{1,0:T(8,128)} async-done(((f32[256,3072]{1,0:T(8,128)}), f32[64,3072]{1,0:T(8,128)}) %reduce-scatter.11.cloned.1.call-update) | async-done | bytes 786448 | tf_op jit(solution)/shard_map/reduce_scatter | solution.py:58
  290.9 40.9 %reduce-scatter.7.cloned.1.call-done = f32[64,3072]{1,0:T(8,128)} async-done(((f32[256,3072]{1,0:T(8,128)}), f32[64,3072]{1,0:T(8,128)}) %reduce-scatter.7.cloned.1.call-update) | async-done | bytes 786448 | tf_op jit(solution)/shard_map/reduce_scatter | solution.py:38
  331.7 3.8 fusion.9
  335.6 0.0 all-gather.11.cloned.1.call-update
  335.6 0.0 all-gather.7.cloned.1.call-start
  335.6 0.5 all-gather.7.cloned.1.call-update
  336.2 0.0 reduce-scatter.13.cloned.1.call-start
  336.2 19.2 %all-gather.11.cloned.1.call-done = bf16[256,3072]{1,0:T(8,128)(2,1)} async-done(((bf16[64,3072]{1,0:T(8,128)(2,1)}), bf16[256,3072]{1,0:T(8,128)(2,1)}) %all-gather.11.cloned.1.call-update) | async-done | bytes 1572880 | tf_op jit(solution)/shard_map/all_gather | solution.py:62
  355.4 8.0 %fusion.20 = f32[256,1536]{1,0:T(8,128)} fusion(bf16[256,3072]{1,0:T(8,128)(2,1)} %all-gather.11.cloned.1.call-done, bf16[1536,3072]{1,0:T(8,128)(2,1)} %all-gather.5.cloned.1.call-done), kind=kOutput, calls=%fused_computation.32 | convolution fusion | flops 2415919104 | bytes 12582912 | tf_op jit(solution)/shard_map/dot_general | solution.py:16
  363.3 0.0 reduce-scatter.13.cloned.1.call-update
  363.4 0.0 reduce-scatter.9.cloned.1.call-start
  363.4 13.6 %all-gather.7.cloned.1.call-done = bf16[256,3072]{1,0:T(8,128)(2,1)} async-done(((bf16[64,3072]{1,0:T(8,128)(2,1)}), bf16[256,3072]{1,0:T(8,128)(2,1)}) %all-gather.7.cloned.1.call-update) | async-done | bytes 1572880 | tf_op jit(solution)/shard_map/all_gather | solution.py:45
  377.0 7.9 %fusion.18 = f32[256,1536]{1,0:T(8,128)} fusion(bf16[256,3072]{1,0:T(8,128)(2,1)} %all-gather.7.cloned.1.call-done, bf16[3072,1536]{1,0:T(8,128)(2,1)} %all-gather.9.cloned.1.call-done), kind=kOutput, calls=%fused_computation.30 | convolution fusion | flops 2415919104 | bytes 12582912 | tf_op jit(solution)/shard_map/dot_general | solution.py:47
  384.9 0.0 reduce-scatter.9.cloned.1.call-update
  385.0 0.0 copy-start.2
  385.0 0.0 reduce-scatter.17.cloned.1.call-start
  385.0 6.8 multiply_convert_fusion
  391.8 0.0 reduce-scatter.17.cloned.1.call-update
  391.8 0.2 reduce-scatter.15.cloned.1.call-start
  392.0 0.0 copy-done.2
  392.0 5.2 fusion
  397.2 0.0 reduce-scatter.15.cloned.1.call-update
  397.3 17.5 %reduce-scatter.13.cloned.1.call-done = f32[64,1536]{1,0:T(8,128)} async-done(((f32[256,1536]{1,0:T(8,128)}), f32[64,1536]{1,0:T(8,128)}) %reduce-scatter.13.cloned.1.call-update) | async-done | bytes 393232 | tf_op jit(solution)/shard_map/reduce_scatter | solution.py:63
  414.8 1.7 convert_element_type.30
  416.5 34.9 %reduce-scatter.9.cloned.1.call-done = f32[64,1536]{1,0:T(8,128)} async-done(((f32[256,1536]{1,0:T(8,128)}), f32[64,1536]{1,0:T(8,128)}) %reduce-scatter.9.cloned.1.call-update) | async-done | bytes 393232 | tf_op jit(solution)/shard_map/reduce_scatter | solution.py:46
  451.4 1.7 convert_element_type.28
  453.1 110.7 %reduce-scatter.17.cloned.1.call-done = bf16[1536,1536]{1,0:T(8,128)(2,1)} async-done(((bf16[3072,1536]{1,0:T(8,128)(2,1)}), bf16[1536,1536]{1,0:T(8,128)(2,1)}) %reduce-scatter.17.cloned.1.call-update) | async-done | bytes 4718608 | tf_op jit(solution)/shard_map/reduce_scatter | solution.py:52
  563.8 7.4 %convert_element_type.35 = f32[1536,1536]{1,0:T(8,128)} convert(bf16[1536,1536]{1,0:T(8,128)(2,1)} %reduce-scatter.17.cloned.1.call-done) | non-fusion elementwise | flops 2359296 | bytes 14155776 | tf_op jit(solution)/shard_map/convert_element_type | solution.py:57
  571.2 106.0 %reduce-scatter.15.cloned.1.call-done = bf16[1536,1536]{0,1:T(8,128)(2,1)} async-done(((bf16[1536,3072]{0,1:T(8,128)(2,1)}), bf16[1536,1536]{0,1:T(8,128)(2,1)}) %reduce-scatter.15.cloned.1.call-update) | async-done | bytes 4718608 | tf_op jit(solution)/shard_map/reduce_scatter | solution.py:67
  677.2 7.4 %copy.8 = f32[1536,1536]{1,0:T(8,128)} copy(bf16[1536,1536]{0,1:T(8,128)(2,1)} %reduce-scatter.15.cloned.1.call-done) | data formatting | bytes 14155776
Async XLA Ops:
  7.2 1.5 copy-start
  7.2 123.1 %all-gather.9.cloned.1.call-start = ((), (), s32[]{:S(2)}) async-start(), calls=%async_computation.9 | async-start | bytes 14155776 | tf_op jit(solution)/shard_map/all_gather | solution.py:34
  7.9 241.9 %all-gather.5.cloned.1.call-start = ((), (), s32[]{:S(2)}) async-start(), calls=%async_computation.6 | async-start | bytes 14155776 | tf_op jit(solution)/shard_map/all_gather | solution.py:33
  8.7 282.2 %reduce-scatter.11.cloned.1.call-start = ((), (), s32[]{:S(2)}) async-start(), calls=%async_computation.11 | async-start | bytes 3932160 | tf_op jit(solution)/shard_map/reduce_scatter | solution.py:58
  30.0 108.3 %copy-start.1 = (bf16[64,1536]{1,0:T(8,128)(2,1)S(1)}, bf16[64,1536]{1,0:T(8,128)(2,1)}, u32[]{:S(2)}) copy-start(bf16[64,1536]{1,0:T(8,128)(2,1)} %param.4) | copy-start | bytes 589828
  138.3 193.4 %reduce-scatter.7.cloned.1.call-start = ((), (), s32[]{:S(2)}) async-start(), calls=%async_computation.7 | async-start | bytes 3932160 | tf_op jit(solution)/shard_map/reduce_scatter | solution.py:38
  257.8 97.6 %all-gather.11.cloned.1.call-start = ((), (), s32[]{:S(2)}) async-start(), calls=%async_computation.12 | async-start | bytes 1966080 | tf_op jit(solution)/shard_map/all_gather | solution.py:62
  335.6 41.5 %all-gather.7.cloned.1.call-start = ((), (), s32[]{:S(2)}) async-start(), calls=%async_computation.8 | async-start | bytes 1966080 | tf_op jit(solution)/shard_map/all_gather | solution.py:45
  336.2 78.6 %reduce-scatter.13.cloned.1.call-start = ((), (), s32[]{:S(2)}) async-start(), calls=%async_computation.13 | async-start | bytes 1966080 | tf_op jit(solution)/shard_map/reduce_scatter | solution.py:63
  363.4 88.1 %reduce-scatter.9.cloned.1.call-start = ((), (), s32[]{:S(2)}) async-start(), calls=%async_computation.10 | async-start | bytes 1966080 | tf_op jit(solution)/shard_map/reduce_scatter | solution.py:46
  385.0 7.1 %copy-start.2 = (bf16[256,3072]{1,0:T(8,128)(2,1)S(1)}, bf16[256,3072]{1,0:T(8,128)(2,1)}, u32[]{:S(2)}) copy-start(bf16[256,3072]{1,0:T(8,128)(2,1)} %all-gather.11.cloned.1.call-done) | copy-start | bytes 4718596
  385.0 178.8 %reduce-scatter.17.cloned.1.call-start = ((), (), s32[]{:S(2)}) async-start(), calls=%async_computation.15 | async-start | bytes 14155776 | tf_op jit(solution)/shard_map/reduce_scatter | solution.py:52
  391.8 285.4 %reduce-scatter.15.cloned.1.call-start = ((), (), s32[]{:S(2)}) async-start(), calls=%async_computation.14 | async-start | bytes 14155776 | tf_op jit(solution)/shard_map/reduce_scatter | solution.py:67
Sparse Core Ops, SparseCore 0:
  9.5 120.6 all-gather.8
  131.8 117.9 all-gather.4
  252.9 37.8 reduce-scatter.10
  293.8 37.8 reduce-scatter.6
  335.7 19.6 all-gather.10
  357.4 19.6 all-gather.6
  379.3 35.4 reduce-scatter.12
  417.1 34.2 reduce-scatter.8
  454.3 109.4 reduce-scatter.16
  566.5 110.6 reduce-scatter.14
where the time goes:
time: 692 us; the launch traced here: 691 us
  waiting for transfers between devices  570 us (82%)
  matrix products  43.7 us (6%)
  blocking collectives  40.9 us (6%)
  other arithmetic  14.6 us (2%)
  between operations  14.2 us (2%)
  local copies, waits for them, and re-layouts  7.41 us (1%)
    reduce_scatter x1, waiting for transfers between devices, per_device(): lax.psum_scatter((contract_first(act_all, grad_rows) * block_scale).astyp...  111 us
    reduce_scatter x1, waiting for transfers between devices, per_device(): lax.psum_scatter(win_term.astype(jnp.bfloat16), 'gx', scatter_dimension=1...  106 us
    all_gather x1, waiting for transfers between devices, per_device(): lax.all_gather(w_out, 'gx', axis=0, tiled=True)  100 us
    all_gather x1, waiting for transfers between devices, per_device(): lax.all_gather(w_in, 'gx', axis=1, tiled=True)  91.9 us
    reduce_scatter x1, waiting for transfers between devices, per_device(): lax.psum_scatter(jnp.dot(tok_rows, win_tile, preferred_element_type=jnp.f...  40.9 us
    reduce_scatter x1, waiting for transfers between devices, per_device(): lax.psum_scatter(jnp.dot(act_all, wout_tile, preferred_element_type=jnp.f...  34.9 us
    reduce_scatter x1, waiting for transfers between devices, per_device(): lax.psum_scatter(contract_last(grad_rows, wout_tile), 'gz', scatter_dimen...  33 us
    all_gather x1, blocking collectives, per_device(): lax.all_gather(grad_out, 'gy', axis=0, tiled=True)  21.3 us
  transfers between devices with their start and end apart: 10, of which 10 were waited for; matrix products, arithmetic and copies ran while one was open for 8% of the time, Pallas kernels for 0%

commit v1 on v0

v1 whole, which is shorter than its diff:
```python
import functools
import math

import jax
import jax.numpy as jnp
from jax import lax
from jax.experimental import pallas as pl
from jax.experimental.pallas import tpu as pltpu
from jax.sharding import PartitionSpec as P

MESH = pl.DeviceIdType.MESH
F32, BF16 = jnp.float32, jnp.bfloat16


def contract(left, right, dims):
    return lax.dot_general(left, right, (dims, ((), ())), preferred_element_type=F32)


def ring_kernel(
    nx, ny, nz,
    tok_ref, grad_ref, win_ref, wout_ref,
    mlp_ref, tgrad_ref, tok_out, grad_out, act_out, dpre_out,
    rows_all, win, wout, part, part_in, hid_all, send_out, own, fold_in, fold, last_in,
    local, a_z, a_x, b_sem, c_sem, d_x, d_z,
):
    x, y, z = lax.axis_index("gx"), lax.axis_index("gy"), lax.axis_index("gz")
    t, width = tok_ref.shape
    hidden = win_ref.shape[1]
    rows = ny * t
    slab = rows // nz
    sends = []

    def block(e):
        return lax.rem(x - e + nx, nx)

    def peer(me, d, n):
        return lax.rem(me + d, n)

    def source(me, d, n):
        return lax.rem(me - d + n, n)

    def remote(src, dst, sems, index, device):
        return pltpu.make_async_remote_copy(
            src_ref=src, dst_ref=dst, send_sem=sems.at[(0, *index)],
            recv_sem=sems.at[(1, *index)], device_id=device, device_id_type=MESH,
        )

    def send(*args):
        copy = remote(*args)
        copy.start()
        sends.append(copy)

    stage = [
        pltpu.make_async_copy(tok_ref, rows_all.at[0, x, y], local.at[0]),
        pltpu.make_async_copy(grad_ref, rows_all.at[1, x, y], local.at[1]),
        pltpu.make_async_copy(win_ref, win, local.at[2]),
        pltpu.make_async_copy(wout_ref, wout, local.at[3]),
    ]
    for copy in stage:
        copy.start()
    barrier = pltpu.get_barrier_semaphore()
    for name, me, n in (("gx", x, nx), ("gy", y, ny), ("gz", z, nz)):
        for d in range(1, n):
            pl.semaphore_signal(
                barrier, inc=1, device_id={name: peer(me, d, n)}, device_id_type=MESH
            )
    pl.semaphore_wait(barrier, nx + ny + nz - 3)

    def across(arr, d):
        slot = rows_all.at[arr, x, source(y, d, ny)]
        for e in range(1, nx):
            send(slot, slot, a_x, (arr, e, d), {"gx": peer(x, e, nx)})

    for arr in range(2):
        stage[arr].wait()
        mine = rows_all.at[arr, x, y]
        for d in range(1, ny):
            send(mine, mine, a_z, (arr, d), {"gy": peer(y, d, ny)})
        across(arr, 0)

    def tiles(size, body):
        tile = 256 if size % 256 == 0 else 128

        def step(i, carry):
            body(pl.ds(pl.multiple_of(i * tile, tile), tile))
            return carry

        lax.fori_loop(0, size // tile, step, 0)

    def project(arr, e):
        left = rows_all.at[arr, block(e)]

        def body(cols):
            lhs = left[...].reshape(rows, width)
            if arr == 0:
                out = contract(lhs, win[:, cols], ((1,), (0,)))
            else:
                out = contract(lhs, wout[cols, :], ((1,), (1,)))
            part[arr, e, :, :, cols] = out.astype(BF16).reshape(nz, slab, -1)

        tiles(hidden, body)
        for d in range(1, nz):
            to = peer(z, d, nz)
            send(part.at[arr, e, to], part_in.at[arr, e, d], b_sem, (arr, e, d), {"gz": to})

    for arr in range(2):
        for d in range(1, ny):
            slot = rows_all.at[arr, x, source(y, d, ny)]
            remote(slot, slot, a_z, (arr, d), {"gy": y}).wait_recv()
            across(arr, d)
        stage[2 + arr].wait()
        project(arr, 0)

    def activate(e):
        for arr in range(2):
            for d in range(1, nz):
                got = part_in.at[arr, e, d]
                remote(got, got, b_sem, (arr, e, d), {"gz": z}).wait_recv()
        g = block(e)

        def body(cols):
            pre, d_act = part[0, e, z, :, cols].astype(F32), part[1, e, z, :, cols].astype(F32)
            for d in range(1, nz):
                pre = pre + part_in[0, e, d, :, cols].astype(F32)
                d_act = d_act + part_in[1, e, d, :, cols].astype(F32)
            cdf = 0.5 * (1.0 + lax.erf(pre * 0.7071067811865476))
            density = jnp.exp(-0.5 * pre * pre) * 0.3989422804014327
            hid_all[0, g, z, :, cols] = (pre * cdf).astype(BF16)
            hid_all[1, g, z, :, cols] = (d_act * (cdf + pre * density)).astype(BF16)

        tiles(hidden, body)
        for arr in range(2):
            mine = hid_all.at[arr, g, z]
            for d in range(1, nz):
                send(mine, mine, c_sem, (arr, e, d), {"gz": peer(z, d, nz)})

    for e in range(1, nx):
        for arr in range(2):
            for d in range(ny):
                slot = rows_all.at[arr, block(e), source(y, d, ny)]
                remote(slot, slot, a_x, (arr, e, d), {"gx": x}).wait_recv()
            project(arr, e)
    stores = [
        pltpu.make_async_copy(rows_all.at[0], tok_out, local.at[4]),
        pltpu.make_async_copy(rows_all.at[1], grad_out, local.at[5]),
    ]
    for copy in stores:
        copy.start()
    order = [*range(1, nx), 0]
    for e in [0, *range(1, nx)]:
        activate(e)

    def expand(arr, e, keep):
        g = block(e)
        for d in range(1, nz):
            got = hid_all.at[arr, g, source(z, d, nz)]
            remote(got, got, c_sem, (arr, e, d), {"gz": z}).wait_recv()
        left = hid_all.at[arr, g]

        def body(cols):
            lhs = left[...].reshape(rows, hidden)
            if arr == 0:
                out = contract(lhs, wout[:, cols], ((1,), (0,)))
            else:
                out = contract(lhs, win[cols, :], ((1,), (1,)))
            if keep:
                own[arr, :, :, cols] = out.reshape(ny, t, -1)
            else:
                send_out[arr, e, :, :, cols] = out.astype(BF16).reshape(ny, t, -1)

        tiles(width, body)
        if not keep:
            send(send_out.at[arr, e], fold_in.at[arr, e], d_x, (arr, e), {"gx": g})

    for e in order:
        for arr in range(2):
            expand(arr, e, e == 0)
    for arr, out in enumerate((act_out, dpre_out)):
        stores.append(pltpu.make_async_copy(hid_all.at[arr], out, local.at[6 + arr]))
        stores[-1].start()
    for arr in range(2):
        for e in range(1, nx):
            got = fold_in.at[arr, e]
            remote(got, got, d_x, (arr, e), {"gx": x}).wait_recv()

        def add(cols, arr=arr):
            total = own[arr, :, :, cols]
            for e in range(1, nx):
                total = total + fold_in[arr, e, :, :, cols].astype(F32)
            own[arr, :, :, cols] = total
            fold[arr, :, :, cols] = total.astype(BF16)

        tiles(width, add)
        for d in range(1, ny):
            to = peer(y, d, ny)
            send(fold.at[arr, to], last_in.at[arr, d], d_z, (arr, d), {"gy": to})
    for arr, out in enumerate((mlp_ref, tgrad_ref)):
        for d in range(1, ny):
            got = last_in.at[arr, d]
            remote(got, got, d_z, (arr, d), {"gy": y}).wait_recv()
        total = own[arr, y]
        for d in range(1, ny):
            total = total + last_in[arr, d].astype(F32)
        out[...] = total.astype(BF16)
    for copy in sends:
        copy.wait_send()
    for copy in stores:
        copy.wait()


def per_device(nx, ny, nz, tokens, grad_out, w_in, w_out):
    t, width = tokens.shape
    hidden = w_in.shape[1]
    rows = ny * t
    slab = rows // nz
    scale = 1.0 / math.sqrt(rows)
    anywhere = pl.BlockSpec(memory_space=pl.ANY)
    vmem = pl.BlockSpec(memory_space=pltpu.VMEM)
    dma = lambda *shape: pltpu.SemaphoreType.DMA((2, *shape))
    shape = jax.ShapeDtypeStruct
    mlp_out, tok_grad, tok_all, grad_all, act_all, d_pre_all = pl.pallas_call(
        functools.partial(ring_kernel, nx, ny, nz),
        out_shape=(
            shape((t, width), BF16), shape((t, width), BF16),
            shape((nx, ny, t, width), BF16), shape((nx, ny, t, width), BF16),
            shape((nx, nz, slab, hidden), BF16), shape((nx, nz, slab, hidden), BF16),
        ),
        in_specs=[anywhere] * 4,
        out_specs=(vmem, vmem, anywhere, anywhere, anywhere, anywhere),
        scratch_shapes=[
            pltpu.VMEM((2, nx, ny, t, width), BF16),
            pltpu.VMEM(w_in.shape, BF16),
            pltpu.VMEM(w_out.shape, BF16),
            pltpu.VMEM((2, nx, nz, slab, hidden), BF16),
            pltpu.VMEM((2, nx, nz, slab, hidden), BF16),
            pltpu.VMEM((2, nx, nz, slab, hidden), BF16),
            pltpu.VMEM((2, nx, ny, t, width), BF16),
            pltpu.VMEM((2, ny, t, width), F32),
            pltpu.VMEM((2, nx, ny, t, width), BF16),
            pltpu.VMEM((2, ny, t, width), BF16),
            pltpu.VMEM((2, ny, t, width), BF16),
            pltpu.SemaphoreType.DMA((8,)),
            dma(2, ny), dma(2, nx, ny), dma(2, nx, nz), dma(2, nx, nz), dma(2, nx), dma(2, ny),
        ],
        compiler_params=pltpu.CompilerParams(
            collective_id=0, has_side_effects=True, vmem_limit_bytes=60 * 2**20
        ),
    )(tokens, grad_out, w_in, w_out)
    tok_all, grad_all = tok_all.reshape(-1, width), grad_all.reshape(-1, width)
    act_all, d_pre_all = act_all.reshape(-1, hidden), d_pre_all.reshape(-1, hidden)
    wout_grad = contract(act_all, grad_all, ((0,), (0,))) * scale
    win_grad = contract(tok_all, d_pre_all, ((0,), (0,))) * scale
    return mlp_out, tok_grad, win_grad, wout_grad


def solution(mesh):
    rows_spec = P(("gx", "gy"), "gz")
    in_spec = P("gz", ("gy", "gx"))
    out_spec = P(("gy", "gx"), "gz")
    sizes = (mesh.shape["gx"], mesh.shape["gy"], mesh.shape["gz"])
    return jax.shard_map(
        functools.partial(per_device, *sizes),
        mesh=mesh,
        in_specs=(rows_spec, rows_spec, in_spec, out_spec),
        out_specs=(rows_spec, rows_spec, in_spec, out_spec),
        check_vma=False,
    )
```

time: 692 us -> 161 us (0.23)
  the two profiles are of different devices: /device:TPU:0 before, /device:TPU:25 now
where the time goes in v1:
time: 161 us
  Pallas kernels  145 us (90%)
  matrix products  13.6 us (8%)
    pallas_call x1, Pallas kernels, per_device(): pl.pallas_call(functools.partial(ring_kernel, nx, ny, nz), out_shape=(sha...  145 us
    dot_general x2, matrix products, contract(): lax.dot_general(left, right, (dims, ((), ())), preferred_element_type=F32)  13.6 us

profile of v1, /device:TPU:25, one launch (start us, length us, event | category | flops | bytes accessed | tf_op | source)
XLA Modules:
  0.0 161.0 jit_solution(16863155689339994722)
XLA Ops:
  0.6 145.3 %shard_map.75 = (bf16[64,1536]{1,0:T(8,128)(2,1)}, bf16[64,1536]{1,0:T(8,128)(2,1)}, bf16[2,4,64,1536]{3,2,1,0:T(8,128)(2,1)}, bf16[2,4,64,1536]{3,2,1,0:T(8,128...) custom-call(bf16[64,1536]{1,0:T(8,128)(2,1)} %tok_ref.1, bf16[64,1536]{1,0:T(8,128)(2,1)} %grad_ref.1, ...), custom_call_target="tpu_custom_call" | custom-call | tf_op jit(solution)/shard_map/pallas_call | solution.py:221
  146.0 0.0 copy-start.2
  146.0 0.0 copy-start.3
  146.0 8.4 %bitcast_multiply_fusion.1 = f32[1536,1536]{1,0:T(8,128)} fusion(bf16[2,4,64,1536]{3,2,1,0:T(8,128)(2,1)} %get-tuple-element.12, bf16[2,4,64,1536]{3,2,1,0:T(8,128)(2,1)} %get-tuple-element.13), kind=kOutput, calls=%fused_computation.1 | convolution fusion | flops 2418278400 | bytes 12582912 | tf_op jit(solution)/shard_map/dot_general | solution.py:16
  154.4 0.0 copy-done.2
  154.4 0.0 copy-done.3
  154.4 0.0 copy-start.1
  154.4 0.0 copy-start
  154.4 5.2 %bitcast_multiply_fusion = f32[1536,1536]{1,0:T(8,128)} fusion(bf16[2,4,64,1536]{3,2,1,0:T(8,128)(2,1)S(1)} %copy-done.3, bf16[2,4,64,1536]{3,2,1,0:T(8,128)(2,1)S(1)} %copy-done.2), kind=kOutput, calls=%fused_computation | convolution fusion | flops 2418278400 | bytes 12582912 | tf_op jit(solution)/shard_map/dot_general | solution.py:16
  159.6 0.0 copy-done.1
  159.6 0.7 copy.12
  160.3 0.0 copy-done
  160.3 0.7 copy.13
Async XLA Ops:
  146.0 8.4 %copy-start.2 = (bf16[2,4,64,1536]{3,2,1,0:T(8,128)(2,1)S(1)}, bf16[2,4,64,1536]{3,2,1,0:T(8,128)(2,1)}, u32[]{:S(2)}) copy-start(bf16[2,4,64,1536]{3,2,1,0:T(8,128)(2,1)} %get-tuple-element.15) | copy-start | bytes 4718596
  146.0 8.4 %copy-start.3 = (bf16[2,4,64,1536]{3,2,1,0:T(8,128)(2,1)S(1)}, bf16[2,4,64,1536]{3,2,1,0:T(8,128)(2,1)}, u32[]{:S(2)}) copy-start(bf16[2,4,64,1536]{3,2,1,0:T(8,128)(2,1)} %get-tuple-element.14) | copy-start | bytes 4718596
  154.4 5.2 %copy-start.1 = (bf16[64,1536]{1,0:T(8,128)(2,1)S(1)}, bf16[64,1536]{1,0:T(8,128)(2,1)}, u32[]{:S(2)}) copy-start(bf16[64,1536]{1,0:T(8,128)(2,1)} %get-tuple-element.20) | copy-start | bytes 589828
  154.4 5.9 %copy-start = (bf16[64,1536]{1,0:T(8,128)(2,1)S(1)}, bf16[64,1536]{1,0:T(8,128)(2,1)}, u32[]{:S(2)}) copy-start(bf16[64,1536]{1,0:T(8,128)(2,1)} %get-tuple-element.21) | copy-start | bytes 589828

commit v2 on v1

--- a/solution.py
+++ b/solution.py
@@ -20,14 +20,18 @@
     nx, ny, nz,
     tok_ref, grad_ref, win_ref, wout_ref,
     mlp_ref, tgrad_ref, tok_out, grad_out, act_out, dpre_out,
-    rows_all, win, wout, part, part_in, hid_all, send_out, own, fold_in, fold, last_in,
-    local, a_z, a_x, b_sem, c_sem, d_x, d_z,
+    rows_all, win, wout, part, pair_in, paired, part_in, hid_all, send_out, own, fold_in, fold, last_in,
+    local, a_z, a_x, p_sem, b_sem, c_sem, d_x, d_z,
 ):
     x, y, z = lax.axis_index("gx"), lax.axis_index("gy"), lax.axis_index("gz")
     t, width = tok_ref.shape
     hidden = win_ref.shape[1]
     rows = ny * t
     slab = rows // nz
+    half = nz // 2
+    core, chip = lax.rem(z, 2), lax.div(z, 2)
+    partner = z + 1 - 2 * core
+    mine_at = core * half + chip
     sends = []
 
     def block(e):
@@ -78,11 +82,11 @@
             send(mine, mine, a_z, (arr, d), {"gy": peer(y, d, ny)})
         across(arr, 0)
 
-    def tiles(size, body):
+    def tiles(size, body, base=0):
         tile = 256 if size % 256 == 0 else 128
 
         def step(i, carry):
-            body(pl.ds(pl.multiple_of(i * tile, tile), tile))
+            body(pl.ds(pl.multiple_of(base + i * tile, 128), tile))
             return carry
 
         lax.fori_loop(0, size // tile, step, 0)
@@ -99,9 +103,24 @@
             part[arr, e, :, :, cols] = out.astype(BF16).reshape(nz, slab, -1)
 
         tiles(hidden, body)
-        for d in range(1, nz):
-            to = peer(z, d, nz)
-            send(part.at[arr, e, to], part_in.at[arr, e, d], b_sem, (arr, e, d), {"gz": to})
+        got = pair_in.at[arr, e]
+        theirs = part.at[arr, e, pl.ds((1 - core) * half, half)]
+        send(theirs, got, p_sem, (arr, e), {"gz": partner})
+        remote(got, got, p_sem, (arr, e), {"gz": z}).wait_recv()
+
+        def join(cols):
+            for d in range(half):
+                total = part[arr, e, core * half + d, :, cols].astype(F32)
+                total = total + pair_in[arr, e, d, :, cols].astype(F32)
+                paired[arr, e, d, :, cols] = total.astype(BF16)
+
+        tiles(hidden, join)
+        for d in range(1, half):
+            to = peer(chip, d, half)
+            send(
+                paired.at[arr, e, to], part_in.at[arr, e, d], b_sem, (arr, e, d),
+                {"gz": 2 * to + core},
+            )
 
     for arr in range(2):
         for d in range(1, ny):
@@ -113,26 +132,35 @@
 
     def activate(e):
         for arr in range(2):
-            for d in range(1, nz):
+            for d in range(1, half):
                 got = part_in.at[arr, e, d]
                 remote(got, got, b_sem, (arr, e, d), {"gz": z}).wait_recv()
         g = block(e)
 
         def body(cols):
-            pre, d_act = part[0, e, z, :, cols].astype(F32), part[1, e, z, :, cols].astype(F32)
-            for d in range(1, nz):
+            pre = paired[0, e, chip, :, cols].astype(F32)
+            d_act = paired[1, e, chip, :, cols].astype(F32)
+            for d in range(1, half):
                 pre = pre + part_in[0, e, d, :, cols].astype(F32)
                 d_act = d_act + part_in[1, e, d, :, cols].astype(F32)
             cdf = 0.5 * (1.0 + lax.erf(pre * 0.7071067811865476))
             density = jnp.exp(-0.5 * pre * pre) * 0.3989422804014327
-            hid_all[0, g, z, :, cols] = (pre * cdf).astype(BF16)
-            hid_all[1, g, z, :, cols] = (d_act * (cdf + pre * density)).astype(BF16)
+            hid_all[0, g, mine_at, :, cols] = (pre * cdf).astype(BF16)
+            hid_all[1, g, mine_at, :, cols] = (d_act * (cdf + pre * density)).astype(BF16)
 
         tiles(hidden, body)
         for arr in range(2):
-            mine = hid_all.at[arr, g, z]
-            for d in range(1, nz):
-                send(mine, mine, c_sem, (arr, e, d), {"gz": peer(z, d, nz)})
+            mine = hid_all.at[arr, g, mine_at]
+            for d in range(1, half):
+                to = peer(chip, d, half)
+                send(mine, mine, c_sem, (arr, e, d), {"gz": 2 * to + core})
+            send(mine, mine, c_sem, (arr, e, 0), {"gz": partner})
+
+    def relay(arr, e):
+        for d in range(1, half):
+            slot = hid_all.at[arr, block(e), core * half + source(chip, d, half)]
+            remote(slot, slot, c_sem, (arr, e, d), {"gz": z}).wait_recv()
+            send(slot, slot, c_sem, (arr, e, half - 1 + d), {"gz": partner})
 
     for e in range(1, nx):
         for arr in range(2):
@@ -149,12 +177,16 @@
     order = [*range(1, nx), 0]
     for e in [0, *range(1, nx)]:
         activate(e)
+    for e in order:
+        for arr in range(2):
+            relay(arr, e)
 
     def expand(arr, e, keep):
         g = block(e)
-        for d in range(1, nz):
-            got = hid_all.at[arr, g, source(z, d, nz)]
-            remote(got, got, c_sem, (arr, e, d), {"gz": z}).wait_recv()
+        for d in range(half):
+            got = hid_all.at[arr, g, (1 - core) * half + source(chip, d, half)]
+            index = half - 1 + d if d else 0
+            remote(got, got, c_sem, (arr, e, index), {"gz": z}).wait_recv()
         left = hid_all.at[arr, g]
 
         def body(cols):
@@ -168,9 +200,14 @@
             else:
                 send_out[arr, e, :, :, cols] = out.astype(BF16).reshape(ny, t, -1)
 
-        tiles(width, body)
-        if not keep:
-            send(send_out.at[arr, e], fold_in.at[arr, e], d_x, (arr, e), {"gx": g})
+        for q in range(2):
+            view = pl.ds(q * (width // 2), width // 2)
+            tiles(width // 2, body, q * (width // 2))
+            if not keep:
+                send(
+                    send_out.at[arr, e, :, :, view], fold_in.at[arr, e, :, :, view],
+                    d_x, (arr, e, q), {"gx": g},
+                )
 
     for e in order:
         for arr in range(2):
@@ -178,26 +215,31 @@
     for arr, out in enumerate((act_out, dpre_out)):
         stores.append(pltpu.make_async_copy(hid_all.at[arr], out, local.at[6 + arr]))
         stores[-1].start()
+    def add(arr, cols):
+        total = own[arr, :, :, cols]
+        for e in range(1, nx):
+            total = total + fold_in[arr, e, :, :, cols].astype(F32)
+        own[arr, :, :, cols] = total
+        fold[arr, :, :, cols] = total.astype(BF16)
+
     for arr in range(2):
-        for e in range(1, nx):
-            got = fold_in.at[arr, e]
-            remote(got, got, d_x, (arr, e), {"gx": x}).wait_recv()
-
-        def add(cols, arr=arr):
-            total = own[arr, :, :, cols]
+        for q in range(2):
+            view = pl.ds(q * (width // 2), width // 2)
             for e in range(1, nx):
-                total = total + fold_in[arr, e, :, :, cols].astype(F32)
-            own[arr, :, :, cols] = total
-            fold[arr, :, :, cols] = total.astype(BF16)
-
-        tiles(width, add)
-        for d in range(1, ny):
-            to = peer(y, d, ny)
-            send(fold.at[arr, to], last_in.at[arr, d], d_z, (arr, d), {"gy": to})
+                got = fold_in.at[arr, e, :, :, view]
+                remote(got, got, d_x, (arr, e, q), {"gx": x}).wait_recv()
+            tiles(width // 2, functools.partial(add, arr), q * (width // 2))
+            for d in range(1, ny):
+                to = peer(y, d, ny)
+                send(
+                    fold.at[arr, to, :, view], last_in.at[arr, d, :, view],
+                    d_z, (arr, d, q), {"gy": to},
+                )
     for arr, out in enumerate((mlp_ref, tgrad_ref)):
         for d in range(1, ny):
-            got = last_in.at[arr, d]
-            remote(got, got, d_z, (arr, d), {"gy": y}).wait_recv()
+            for q in range(2):
+                got = last_in.at[arr, d, :, pl.ds(q * (width // 2), width // 2)]
+                remote(got, got, d_z, (arr, d, q), {"gy": y}).wait_recv()
         total = own[arr, y]
         for d in range(1, ny):
             total = total + last_in[arr, d].astype(F32)
@@ -232,7 +274,9 @@
             pltpu.VMEM(w_in.shape, BF16),
             pltpu.VMEM(w_out.shape, BF16),
             pltpu.VMEM((2, nx, nz, slab, hidden), BF16),
-            pltpu.VMEM((2, nx, nz, slab, hidden), BF16),
+            pltpu.VMEM((2, nx, nz // 2, slab, hidden), BF16),
+            pltpu.VMEM((2, nx, nz // 2, slab, hidden), BF16),
+            pltpu.VMEM((2, nx, nz // 2, slab, hidden), BF16),
             pltpu.VMEM((2, nx, nz, slab, hidden), BF16),
             pltpu.VMEM((2, nx, ny, t, width), BF16),
             pltpu.VMEM((2, ny, t, width), F32),
@@ -240,7 +284,7 @@
             pltpu.VMEM((2, ny, t, width), BF16),
             pltpu.VMEM((2, ny, t, width), BF16),
             pltpu.SemaphoreType.DMA((8,)),
-            dma(2, ny), dma(2, nx, ny), dma(2, nx, nz), dma(2, nx, nz), dma(2, nx), dma(2, ny),
+            dma(2, ny), dma(2, nx, ny), dma(2, nx), dma(2, nx, nz), dma(2, nx, nz), dma(2, nx, 2), dma(2, ny, 2),
         ],
         compiler_params=pltpu.CompilerParams(
             collective_id=0, has_side_effects=True, vmem_limit_bytes=60 * 2**20

time: 161 us -> 140 us (0.87)
  the two profiles are of different devices: /device:TPU:25 before, /device:TPU:0 now
where the time goes in v2:
time: 140 us
  Pallas kernels  124 us (89%)
  matrix products  13.6 us (10%)
    pallas_call x1, Pallas kernels, per_device(): pl.pallas_call(functools.partial(ring_kernel, nx, ny, nz), out_shape=(sha...  124 us
    dot_general x2, matrix products, contract(): lax.dot_general(left, right, (dims, ((), ())), preferred_element_type=F32)  13.6 us

profile of v2, /device:TPU:0, one launch (start us, length us, event | category | flops | bytes accessed | tf_op | source)
XLA Modules:
  0.0 140.0 jit_solution(15650024409753496872)
XLA Ops:
  0.6 124.4 %shard_map.75 = (bf16[64,1536]{1,0:T(8,128)(2,1)}, bf16[64,1536]{1,0:T(8,128)(2,1)}, bf16[2,4,64,1536]{3,2,1,0:T(8,128)(2,1)}, bf16[2,4,64,1536]{3,2,1,0:T(8,128...) custom-call(bf16[64,1536]{1,0:T(8,128)(2,1)} %tok_ref.1, bf16[64,1536]{1,0:T(8,128)(2,1)} %grad_ref.1, ...), custom_call_target="tpu_custom_call" | custom-call | tf_op jit(solution)/shard_map/pallas_call | solution.py:263
  125.0 0.0 copy-start.2
  125.0 0.0 copy-start.3
  125.0 8.4 %bitcast_multiply_fusion.1 = f32[1536,1536]{1,0:T(8,128)} fusion(bf16[2,4,64,1536]{3,2,1,0:T(8,128)(2,1)} %get-tuple-element.12, bf16[2,4,64,1536]{3,2,1,0:T(8,128)(2,1)} %get-tuple-element.13), kind=kOutput, calls=%fused_computation.1 | convolution fusion | flops 2418278400 | bytes 12582912 | tf_op jit(solution)/shard_map/dot_general | solution.py:16
  133.5 0.0 copy-done.2
  133.5 0.0 copy-done.3
  133.5 0.0 copy-start.1
  133.5 0.0 copy-start
  133.5 5.2 %bitcast_multiply_fusion = f32[1536,1536]{1,0:T(8,128)} fusion(bf16[2,4,64,1536]{3,2,1,0:T(8,128)(2,1)S(1)} %copy-done.3, bf16[2,4,64,1536]{3,2,1,0:T(8,128)(2,1)S(1)} %copy-done.2), kind=kOutput, calls=%fused_computation | convolution fusion | flops 2418278400 | bytes 12582912 | tf_op jit(solution)/shard_map/dot_general | solution.py:16
  138.7 0.0 copy-done.1
  138.7 0.7 copy.12
  139.4 0.0 copy-done
  139.4 0.7 copy.13
Async XLA Ops:
  125.0 8.4 %copy-start.2 = (bf16[2,4,64,1536]{3,2,1,0:T(8,128)(2,1)S(1)}, bf16[2,4,64,1536]{3,2,1,0:T(8,128)(2,1)}, u32[]{:S(2)}) copy-start(bf16[2,4,64,1536]{3,2,1,0:T(8,128)(2,1)} %get-tuple-element.15) | copy-start | bytes 4718596
  125.0 8.4 %copy-start.3 = (bf16[2,4,64,1536]{3,2,1,0:T(8,128)(2,1)S(1)}, bf16[2,4,64,1536]{3,2,1,0:T(8,128)(2,1)}, u32[]{:S(2)}) copy-start(bf16[2,4,64,1536]{3,2,1,0:T(8,128)(2,1)} %get-tuple-element.14) | copy-start | bytes 4718596
  133.5 5.2 %copy-start.1 = (bf16[64,1536]{1,0:T(8,128)(2,1)S(1)}, bf16[64,1536]{1,0:T(8,128)(2,1)}, u32[]{:S(2)}) copy-start(bf16[64,1536]{1,0:T(8,128)(2,1)} %get-tuple-element.20) | copy-start | bytes 589828
  133.5 5.9 %copy-start = (bf16[64,1536]{1,0:T(8,128)(2,1)S(1)}, bf16[64,1536]{1,0:T(8,128)(2,1)}, u32[]{:S(2)}) copy-start(bf16[64,1536]{1,0:T(8,128)(2,1)} %get-tuple-element.21) | copy-start | bytes 589828
